TPU v7x, 32 devices: a whole 2x2x4 slice. The times are simulated.
32 devices in a mesh: rays: 2 (over x), freq: 16 (over z, y, core).
Axes of the slice: x: 2, y: 2, z: 4, core: 2. Of those that a mesh axis runs over, the one named last changes fastest.
Arguments:
- spectra: bfloat16 [32, 2, 1024, 1024], P(('rays', 'freq')), parts along dimension 0, may hold values from -6 to 6
- wavelet: float32 [16, 2], P('freq'), may hold values from -6 to 6
- freq_index: int32 [16], P('freq'), may hold values from 0 to 15, each once
- slowness: float32 [16], replicated, may hold values from 0.000222 to 0.000667
- layer_ids: int32 [1], replicated, may hold values from 0 to 15
- ray_slowness: float32 [4], P('rays'), parts along dimension 0, may hold values from -0.0001 to 0.0001
Outputs:
- migrated_image: float32 [2, 1024, 1024], P('rays', 'freq'), parts along dimension 0
There are 2 independent parts, one for each index of `rays`. A program takes and returns all parts, laid end to end along the dimension named above; an argument that names none is the same for every part. Nothing has to cross between parts.
Inputs may be any that keep to these rules, and one draw needn't show every extreme that they name: `freq_index`: each frequency 0 to 15 is held by exactly one slot.
All inputs are finite; a program needn't handle non-finite values.
Results may differ from a plain program's by a relative error of at most 0.0065.
Values sent between devices are 32-bit elements; how exact they have to be, the bound alone decides.
A program may use at most 128 MiB of HBM per device.

v0:
```python
import math

import jax
import jax.numpy as jnp
from jax import lax
from jax.sharding import PartitionSpec as P

GRID_STEP = 12.5
DEPTH_STEP = 10.0
LOW_FREQUENCY = 5.0
FREQUENCY_BAND = 50.0
DAMPING = 6.0
radix_factor = 8


def block_table(length):
    left_side = jnp.arange(length, dtype=jnp.int32)[:, None]
    right_side = jnp.arange(length, dtype=jnp.int32)[None, :]
    angles = (left_side * right_side % length).astype(jnp.float32) * (2.0 * math.pi / length)
    cosines = jnp.cos(angles)
    sines = jnp.sin(angles)
    from_real = jnp.stack([cosines, sines], axis=1)
    from_imag = jnp.stack([-sines, cosines], axis=1)
    return jnp.stack([from_real, from_imag], axis=0).astype(jnp.bfloat16)


def twiddle(length):
    outer_pos = jnp.arange(radix_factor, dtype=jnp.int32)[:, None]
    inner_pos = jnp.arange(length // radix_factor, dtype=jnp.int32)[None, :]
    angles = (outer_pos * inner_pos % length).astype(jnp.float32) * (2.0 * math.pi / length)
    return (jnp.cos(angles), jnp.sin(angles))


def inverse_rows(field, small_table, large_table, twists):
    row_total = field.shape[1]
    column_total = field.shape[2]
    shaped = field.reshape(2, radix_factor, row_total // radix_factor, column_total)
    initial = jnp.einsum("cakx,cadn->dnkx", shaped, small_table, preferred_element_type=jnp.float32)
    cosines, sines = twists
    real_part = initial[0] * cosines[:, :, None] - initial[1] * sines[:, :, None]
    imag_part = initial[0] * sines[:, :, None] + initial[1] * cosines[:, :, None]
    turned = jnp.stack([real_part, imag_part]).astype(jnp.bfloat16)
    second = jnp.einsum("cnkx,ckdm->dmnx", turned, large_table, preferred_element_type=jnp.float32)
    return second.reshape(2, row_total, column_total).astype(jnp.bfloat16)


def inverse_columns(field, small_table, large_table, twists):
    row_total = field.shape[1]
    column_total = field.shape[2]
    shaped = field.reshape(2, row_total, radix_factor, column_total // radix_factor)
    initial = jnp.einsum("crak,cadn->drnk", shaped, small_table, preferred_element_type=jnp.float32)
    cosines, sines = twists
    real_part = initial[0] * cosines[None] - initial[1] * sines[None]
    imag_part = initial[0] * sines[None] + initial[1] * cosines[None]
    turned = jnp.stack([real_part, imag_part]).astype(jnp.bfloat16)
    second = jnp.einsum("crnk,ckdm->drmn", turned, large_table, preferred_element_type=jnp.float32)
    return second.reshape(2, row_total, column_total)


def wavenumbers(length):
    positions = jnp.arange(length, dtype=jnp.int32)
    signed = jnp.where(positions >= length // 2, positions - length, positions)
    return signed.astype(jnp.float32) * (2.0 * math.pi / (length * GRID_STEP))


def phase_factor(angular, layer_slow, wave_square):
    real_arg = (angular * angular - DAMPING * DAMPING) * layer_slow * layer_slow - wave_square
    imag_arg = 2.0 * angular * DAMPING * layer_slow * layer_slow
    modulus = jnp.sqrt(real_arg * real_arg + imag_arg * imag_arg)
    larger = jnp.sqrt(0.5 * (modulus + jnp.abs(real_arg)))
    smaller = imag_arg / (2.0 * larger)
    vertical_real = jnp.where(real_arg >= 0.0, larger, smaller)
    vertical_imag = jnp.where(real_arg >= 0.0, smaller, larger)
    damping_factor = jnp.exp(-vertical_imag * DEPTH_STEP)
    return (
        damping_factor * jnp.cos(vertical_real * DEPTH_STEP),
        damping_factor * jnp.sin(vertical_real * DEPTH_STEP),
    )


def layer_value(slowness, layer_id):
    matches = jnp.arange(slowness.shape[0], dtype=jnp.int32) == layer_id
    return jnp.sum(jnp.where(matches, slowness, jnp.float32(0.0)))


def image_rows(
    row_field, wave_pair, angular, ray_slowness, delay_time, row_count, tables, column_twists
):
    receiver = inverse_columns(row_field, tables[0], tables[2], column_twists)
    column_place = jnp.arange(row_field.shape[2], dtype=jnp.int32).astype(jnp.float32) * GRID_STEP
    row_place = jnp.arange(row_count, dtype=jnp.int32).astype(jnp.float32) * GRID_STEP
    source_phase = angular * (
        ray_slowness[0] * column_place[None, :] + ray_slowness[1] * row_place[:, None] + delay_time
    )
    cos_src = jnp.cos(source_phase)
    sin_src = jnp.sin(source_phase)
    weight_real = wave_pair[0] * cos_src + wave_pair[1] * sin_src
    weight_imag = wave_pair[0] * sin_src - wave_pair[1] * cos_src
    return weight_real * receiver[0] - weight_imag * receiver[1]


def body(spectra, wavelet, freq_index, slowness, layer_ids, ray_slowness):
    slot_total = spectra.shape[0]
    row_total = spectra.shape[2]
    column_total = spectra.shape[3]
    groups = lax.axis_size("freq")
    freq_total = slot_total * groups
    wave_y = wavenumbers(row_total)
    wave_x = wavenumbers(column_total)
    wave_square = wave_y[:, None] * wave_y[:, None] + wave_x[None, :] * wave_x[None, :]
    tables = (
        block_table(radix_factor),
        block_table(row_total // radix_factor),
        block_table(column_total // radix_factor),
    )
    row_twists = twiddle(row_total)
    column_twists = twiddle(column_total)
    angulars = (freq_index.astype(jnp.float32) * (FREQUENCY_BAND / freq_total) + LOW_FREQUENCY) * (
        2.0 * math.pi
    )
    spectrums = [spectra[0].astype(jnp.float32)]
    delay_time = jnp.float32(0.0)
    layer_slow = layer_value(slowness, layer_ids[0])
    vertical = jnp.sqrt(
        layer_slow * layer_slow
        - ray_slowness[0] * ray_slowness[0]
        - ray_slowness[1] * ray_slowness[1]
    )
    delay_time = vertical * DEPTH_STEP
    cos_part, sin_part = phase_factor(angulars[0], layer_slow, wave_square)
    spectrum = spectrums[0]
    real_new = spectrum[0] * cos_part - spectrum[1] * sin_part
    imag_new = spectrum[0] * sin_part + spectrum[1] * cos_part
    spectrums[0] = jnp.stack([real_new, imag_new])
    energy_local = jnp.sum(real_new * real_new + imag_new * imag_new)
    row_fields = inverse_rows(spectrums[0].astype(jnp.bfloat16), tables[0], tables[1], row_twists)
    energy_total = lax.psum(energy_local, "freq")
    energy_scale = 1.0 / jnp.sqrt(energy_total / freq_total + 1e-06)
    summed = image_rows(
        row_fields,
        wavelet[0],
        angulars[0],
        ray_slowness,
        delay_time,
        row_total // groups * lax.axis_size("freq"),
        tables,
        column_twists,
    )
    reduced = lax.psum_scatter(summed, "freq", scatter_dimension=0, tiled=True)
    images = [reduced * energy_scale]
    return jnp.stack(images)


def solution(mesh):
    placed = (
        P(("rays", "freq"), None, None, None),
        P("freq", None),
        P("freq"),
        P(),
        P(),
        P("rays"),
    )
    return jax.shard_map(
        body, mesh=mesh, in_specs=placed, out_specs=P("rays", "freq", None), check_vma=False
    )
```

profile of v0, /device:TPU:0, one launch (start us, length us, event | category | flops | bytes accessed | tf_op | source)
XLA Modules:
  0.0 193.2 jit_solution(3707752803091987818)
XLA Ops:
  6.5 0.0 reduce-scatter.4.cloned.1.call-start
  6.5 1.3 fusion.62
  11.9 0.1 fusion.54
  11.9 0.1 negate_convert_fusion.1
  12.0 0.1 fusion.51
  12.0 0.3 fusion.35
  12.3 0.3 negate_convert_fusion
  13.9 1.3 fusion.55
  18.5 1.3 fusion.61
  19.9 0.1 copy.43
  20.0 0.1 copy.44
  20.1 0.1 copy.48
  20.2 0.1 copy.47
  20.3 3.2 %convert_element_type.134 = f32[1,2,1024,1024]{3,2,1,0:T(8,128)S(1)} convert(bf16[1,2,1024,1024]{3,2,1,0:T(8,128)(2,1)} %param.6) | non-fusion elementwise | flops 2097152 | bytes 12582912 | tf_op jit(solution)/shard_map/convert_element_type | solution.py:121
  23.5 0.0 copy-start
  23.5 21.9 %fusion.15 = (bf16[1,1024,1024]{2,1,0:T(8,128)(2,1)S(1)}, bf16[1,1024,1024]{2,1,0:T(8,128)(2,1)S(1)}) fusion(f32[1,2,1024,1024]{3,2,1,0:T(8,128)S(1)} %convert_element_type.134, f32[]{:T(128)S(6)} %mul.666, f32[]{:T(128)S(6)} %mul.664, f32[1024]{0:T(1024)S(1)} %fusion.44, f32[]{:T(128)S(6)} %mul.659), kind=kLoop, calls=%fused_computation.27 | loop fusion | flops 26214400 | bytes 12591116 | tf_op jit(solution)/shard_map/convert.7
  45.5 0.0 copy-done
  45.5 1.2 copy.45
  46.6 1.2 copy.46
  47.8 1.3 fusion.25
  49.1 1.4 subtract_convert_fusion.1
  50.5 0.4 pad_maximum_fusion
  50.9 5.2 %bitcast_convert_fusion = bf16[2,128,8,1024]{3,1,2,0:T(8,128)(2,1)S(1)} fusion(bf16[2,8,128,1024]{3,1,2,0:T(8,128)(2,1)S(1)} %pad_maximum_fusion, bf16[1,128,2,128]{1,3,0,2:T(8,128)(2,1)S(1)} %get-tuple-element.14, bf16[1,128,2,128]{1,3,0,2:T(8,128)(2,1)S(1)} %get-tuple-element.13), kind=kOutput, calls=%fused_computation | convolution fusion | flops 1076101120 | bytes 8519680 | tf_op jit(solution)/shard_map/cnkx,ckdm->dmnx/dot_general | solution.py:43
  56.1 6.3 %copy.62 = bf16[2,128,8,1024]{3,0,2,1:T(2,128)(2,1)} copy(bf16[2,128,8,1024]{3,1,2,0:T(8,128)(2,1)S(1)} %bitcast_convert_fusion) | data formatting | bytes 8388608 | tf_op jit(solution)/shard_map/convert_element_type | solution.py:44
  62.4 7.6 %reshape.439 = bf16[2,1024,8,128,1]{3,2,0,1,4:T(8,128)(2,1)} reshape(bf16[2,128,8,1024]{3,0,2,1:T(2,128)(2,1)} %copy.62) | data formatting | bytes 8388608 | tf_op jit(solution)/shard_map/convert_element_type | solution.py:44
  70.0 3.5 %convolution_bitcast_fusion = f32[2,1024,8,128]{3,2,1,0:T(8,128)S(1)} fusion(bf16[2,1024,8,128,1]{3,2,0,1,4:T(8,128)(2,1)} %reshape.439, bf16[1,8,2,8]{1,3,0,2:T(8,128)(2,1)S(1)} %copy.44, bf16[1,8,2,8]{1,3,0,2:T(8,128)(2,1)S(1)} %copy.43), kind=kOutput, calls=%fused_computation.50 | convolution fusion | flops 67109888 | bytes 12583424 | tf_op jit(solution)/shard_map/crak,cadn->drnk/dot_general | solution.py:51
  73.5 1.1 subtract_convert_fusion
  74.6 0.4 pad_maximum_fusion.1
  75.0 1.4 fusion.22
  76.4 4.1 %fusion.60 = (f32[1,1024,128,8]{1,2,3,0:T(8,128)}, f32[1,1024,128,8]{1,2,3,0:T(8,128)}) fusion(f32[2,1024,128,8]{1,2,3,0:T(8,128)S(1)} %fusion.22), kind=kLoop, calls=%fused_computation.107 | loop fusion | bytes 16777216 | tf_op jit(solution)/shard_map/slice | solution.py:99
  80.4 22.4 %fusion.9 = f32[1024,1024]{0,1:T(8,128)} fusion(f32[1,1024,128,8]{1,2,3,0:T(8,128)} %get-tuple-element.12, f32[1,1024,128,8]{1,2,3,0:T(8,128)} %get-tuple-element.11, f32[]{:T(128)} %bitcast.7, f32[]{:T(128)S(6)} %mul.643, f32[1024]{0:T(1024)S(1)} %get-tuple-element.27, f32[1024]{0:T(1024)S(1)} %get-tuple-element.28, f32[]{:T(128)} %bitcast.1, f32[]{:T(128)} %bitcast), kind=kLoop, calls=%fused_computation.18 | loop fusion | flops 12582912 | bytes 12591120 | tf_op jit(solution)/shard_map/sub | solution.py:99
  102.8 5.4 %copy.63 = f32[1024,1024]{1,0:T(8,128)} copy(f32[1024,1024]{0,1:T(8,128)} %fusion.9) | data formatting | bytes 8388608
  108.2 0.0 reduce-scatter.4.cloned.1.call-update
  108.2 23.6 %fusion.6 = f32[]{:T(128)} fusion(f32[1,2,1024,1024]{3,2,1,0:T(8,128)} %copy-done, f32[]{:T(128)S(6)} %mul.666, f32[]{:T(128)S(6)} %mul.664, f32[1024]{0:T(1024)S(1)} %fusion.44, f32[]{:T(128)S(6)} %mul.659), kind=kLoop, calls=%fused_computation.12 | loop fusion | flops 28311552 | bytes 8396816 | tf_op jit(solution)/shard_map/reduce_sum | solution.py:135
  131.8 36.0 %psum.7 = f32[]{:T(128)} all-reduce(f32[]{:T(128)} %fusion.6), channel_id=1, replica_groups=mesh['rays'=2,'freq'=16] {'freq'}, use_global_device_ids=true, to_apply=%region_3.4 | all-reduce | flops 1 | bytes 8 | tf_op jit(solution)/shard_map/psum | solution.py:137
  168.5 15.8 %reduce-scatter.4.cloned.1.call-done = f32[64,1024]{1,0:T(8,128)} async-done(((f32[1024,1024]{1,0:T(8,128)}), f32[64,1024]{1,0:T(8,128)}) %reduce-scatter.4.cloned.1.call-update) | async-done | bytes 262160
  184.3 1.1 copy.64
  185.5 0.9 copy.55
  (5 shorter events, 0.1 us)
Async XLA Ops:
  6.5 177.7 %reduce-scatter.4.cloned.1.call-start = ((), (), s32[]{:S(2)}) async-start(), calls=%async_computation.1 | async-start | bytes 4456448
  23.5 22.0 %copy-start = (f32[1,2,1024,1024]{3,2,1,0:T(8,128)}, f32[1,2,1024,1024]{3,2,1,0:T(8,128)S(1)}, u32[]{:S(2)}) copy-start(f32[1,2,1024,1024]{3,2,1,0:T(8,128)S(1)} %convert_element_type.134) | copy-start | bytes 25165828
Sparse Core Ops, SparseCore 0:
  108.3 75.9 reduce-scatter.3
where the time goes:
time: 194 us; the launch traced here: 193 us
  other arithmetic  76.4 us (39%)
  blocking collectives  36 us (19%)
  local copies, waits for them, and re-layouts  30.7 us (16%)
  between operations  23 us (12%)
  waiting for transfers between devices  15.8 us (8%)
  matrix products  11.3 us (6%)
    psum x1, blocking collectives, body(): energy_total = lax.psum(energy_local, 'freq')  36 us
    another operation x7, other arithmetic  25.1 us
    reduce_sum x1, other arithmetic, body(): energy_local = jnp.sum(real_new * real_new + imag_new * imag_new)  23.6 us
    sub x1, other arithmetic, image_rows(): return weight_real * receiver[0] - weight_imag * receiver[1]  22.4 us
    unnamed x2, waiting for transfers between devices  15.8 us
    convert_element_type x2, local copies, waits for them, and re-layouts, inverse_rows(): return second.reshape(2, row_total, column_total).astype(jnp.bfloat16)  13.9 us
    unnamed x4, local copies, waits for them, and re-layouts  6.5 us
    dot_general x1, matrix products, inverse_rows(): jnp.einsum('cnkx,ckdm->dmnx', turned, large_table, preferred_element_type...  5.2 us
  transfers between devices with their start and end apart: 1, of which 1 were waited for; matrix products, arithmetic and copies ran while one was open for 12% of the time, Pallas kernels for 0%

commit v1 on v0

v1 whole, which is shorter than its diff:
```python
import functools
import math

import jax
import jax.numpy as jnp
from jax import lax
from jax.experimental import pallas as pl
from jax.experimental.pallas import tpu as pltpu
from jax.sharding import PartitionSpec as P

GRID_STEP = 12.5
DEPTH_STEP = 10.0
LOW_FREQUENCY = 5.0
FREQUENCY_BAND = 50.0
DAMPING = 6.0
X_RADIX = 8
LANES = 128
MESH = pl.DeviceIdType.MESH

SIN_COEFS = [(-1.0) ** i / math.factorial(2 * i + 1) for i in range(6)]
COS_COEFS = [(-1.0) ** i / math.factorial(2 * i) for i in range(7)]


def half_sincos(half):
    square = half * half
    sine = jnp.full_like(square, SIN_COEFS[-1])
    for coef in SIN_COEFS[-2::-1]:
        sine = sine * square + coef
    sine = sine * half
    cosine = jnp.full_like(square, COS_COEFS[-1])
    for coef in COS_COEFS[-2::-1]:
        cosine = cosine * square + coef
    twice = sine + sine
    return twice * cosine, 1.0 - twice * sine


def turn_sincos(turns):
    reduced = turns - jnp.floor(turns + 0.5)
    return half_sincos(reduced * math.pi)


def butterfly(parts):
    count = len(parts)
    if count == 1:
        return parts
    even = butterfly(parts[0::2])
    odd = butterfly(parts[1::2])
    low, high = [], []
    for i in range(count // 2):
        er, ei = even[i]
        xr, xi = odd[i]
        if i == 0:
            tr, ti = xr, xi
        elif 4 * i == count:
            tr, ti = -xi, xr
        elif 8 * i == count:
            root = math.sqrt(0.5)
            tr, ti = (xr - xi) * root, (xr + xi) * root
        elif 8 * i == 3 * count:
            root = math.sqrt(0.5)
            tr, ti = (xr + xi) * -root, (xr - xi) * root
        else:
            c = math.cos(2 * math.pi * i / count)
            s = math.sin(2 * math.pi * i / count)
            tr, ti = xr * c - xi * s, xr * s + xi * c
        low.append((er + tr, ei + ti))
        high.append((er - tr, ei - ti))
    return low + high


def kernel(
    groups, radix, pieces,
    scal, spec_hbm, out_ref,
    spec, zed, ytab, field, xtab, vecs, image, core_in, pair_in, low_in, high_in, etile, eall,
    load_sem, core_s, core_r, pair_s, pair_r, low_s, low_r, high_s, high_r, e_s, e_r,
):
    rows = spec.shape[1] * spec.shape[2]
    cols = spec.shape[3]
    short = rows // radix
    lines = groups // 4
    me = lax.axis_index("freq")
    core = lax.rem(me, 2)
    pair = lax.rem(me // 2, 2)
    spot = me // 4
    core_peer = me + 1 - 2 * core
    pair_peer = me + 2 - 4 * pair

    barrier = pltpu.get_barrier_semaphore()

    def greet(i, carry):
        pl.semaphore_signal(
            barrier, inc=1, device_id={"freq": lax.rem(me + i, groups)}, device_id_type=MESH
        )
        return carry

    lax.fori_loop(1, groups, greet, 0)

    strips = short // 16
    tiles = cols // LANES

    def load(i):
        window = pl.ds(pl.multiple_of(i * 16, 16), 16)
        return pltpu.make_async_copy(
            spec_hbm.at[:, :, window, :], spec.at[:, :, window, :], load_sem.at[i]
        )

    def start_load(i, carry):
        load(i).start()
        return carry

    lax.fori_loop(0, strips, start_load, 0)

    real_base = scal[0]
    imag_arg = scal[1]
    turn_x = scal[2]
    turn_y = scal[3]
    turn_0 = scal[4]
    wave_re = scal[5]
    wave_im = scal[6]
    freq_total = scal[7]

    block = cols // X_RADIX
    place = lax.broadcasted_iota(jnp.int32, (X_RADIX, cols), 1)
    outer = lax.broadcasted_iota(jnp.int32, (X_RADIX, cols), 0)
    eighth = lax.rem(place * outer, X_RADIX).astype(jnp.float32) * (1.0 / X_RADIX)
    vec_sin, vec_cos = turn_sincos(eighth + place.astype(jnp.float32) * turn_x)
    vecs[0] = vec_cos
    vecs[1] = vec_sin

    def x_table(step, carry):
        strip = step // tiles
        tile = lax.rem(step, tiles)
        at = pl.ds(pl.multiple_of(tile * LANES, LANES), LANES)
        k = lax.broadcasted_iota(jnp.int32, (16, LANES), 0) + strip * 16
        x = lax.broadcasted_iota(jnp.int32, (16, LANES), 1) + tile * LANES
        turns = lax.rem(k * x, cols).astype(jnp.float32) * (1.0 / cols)
        sine, cosine = turn_sincos(turns)
        for k1 in range(X_RADIX):
            vc = vecs[0, k1 : k1 + 1, at]
            vs = vecs[1, k1 : k1 + 1, at]
            row = pl.ds(pl.multiple_of(strip * 16 + k1 * block, 16), 16)
            row_im = pl.ds(pl.multiple_of(strip * 16 + k1 * block + cols, 16), 16)
            xtab[row, at] = (cosine * vc - sine * vs).astype(jnp.bfloat16)
            xtab[row_im, at] = (-(cosine * vs) - sine * vc).astype(jnp.bfloat16)
        return carry

    lax.fori_loop(0, (block // 16) * tiles, x_table, 0)

    ytiles = short // LANES

    def y_table(step, carry):
        n1 = step // (strips * ytiles)
        strip = lax.rem(step // ytiles, strips)
        tile = lax.rem(step, ytiles)
        n2 = lax.broadcasted_iota(jnp.int32, (16, LANES), 0) + strip * 16
        k2 = lax.broadcasted_iota(jnp.int32, (16, LANES), 1) + tile * LANES
        n = n2 * radix + n1
        turns = lax.rem(k2 * n, rows).astype(jnp.float32) * (1.0 / rows)
        sine, cosine = turn_sincos(turns + n.astype(jnp.float32) * turn_y + turn_0)
        real = (wave_re * cosine + wave_im * sine).astype(jnp.bfloat16)
        imag_f = wave_re * sine - wave_im * cosine
        imag = imag_f.astype(jnp.bfloat16)
        top = pl.ds(pl.multiple_of(strip * 16, 16), 16)
        bottom = pl.ds(pl.multiple_of(strip * 16 + short, 16), 16)
        left = pl.ds(pl.multiple_of(tile * LANES, LANES), LANES)
        right = pl.ds(pl.multiple_of(tile * LANES + short, LANES), LANES)
        ytab[n1, top, left] = real
        ytab[n1, top, right] = (-imag_f).astype(jnp.bfloat16)
        ytab[n1, bottom, left] = imag
        ytab[n1, bottom, right] = real
        return carry

    lax.fori_loop(0, radix * strips * ytiles, y_table, 0)

    step_y = 2.0 * math.pi / (rows * GRID_STEP)
    step_x = 2.0 * math.pi / (cols * GRID_STEP)
    imag_sq = imag_arg * imag_arg
    imag_half = imag_arg * 0.5

    def shift(strip, total):
        load(strip).wait()
        rows_at = pl.ds(pl.multiple_of(strip * 16, 16), 16)

        def inner(tile, acc):
            at = pl.ds(pl.multiple_of(tile * LANES, LANES), LANES)
            kx = lax.broadcasted_iota(jnp.int32, (16, LANES), 1) + tile * LANES
            kx = jnp.where(kx >= cols // 2, kx - cols, kx).astype(jnp.float32) * step_x
            base = real_base - kx * kx
            sub = lax.broadcasted_iota(jnp.int32, (16, LANES), 0) + strip * 16
            parts = []
            for k1 in range(radix):
                offset = k1 * short - (rows if k1 >= radix // 2 else 0)
                ky = (sub + offset).astype(jnp.float32) * step_y
                a = base - ky * ky
                m = a * a + imag_sq
                q = 0.5 * (m * lax.rsqrt(m) + jnp.abs(a))
                iq = lax.rsqrt(q)
                g = q * iq
                h = imag_half * iq
                forward = a >= 0.0
                vert_re = jnp.where(forward, g, h)
                vert_im = jnp.where(forward, h, g)
                damp = jnp.exp(vert_im * -DEPTH_STEP)
                sine, cosine = half_sincos(vert_re * (0.5 * DEPTH_STEP))
                cosine = cosine * damp
                sine = sine * damp
                re = spec[0, k1, rows_at, at].astype(jnp.float32)
                im = spec[1, k1, rows_at, at].astype(jnp.float32)
                new_re = re * cosine - im * sine
                new_im = re * sine + im * cosine
                acc = acc + (new_re * new_re + new_im * new_im)
                parts.append((new_re, new_im))
            for n1, (re, im) in enumerate(butterfly(parts)):
                zed[n1, rows_at, at] = re.astype(jnp.bfloat16)
                low = pl.ds(pl.multiple_of(strip * 16 + short, 16), 16)
                zed[n1, low, at] = im.astype(jnp.bfloat16)
            return acc

        return lax.fori_loop(0, tiles, inner, total)

    energy = lax.fori_loop(0, strips, shift, jnp.zeros((16, LANES), jnp.float32))
    etile[...] = energy[:8] + energy[8:]

    chips = groups // 2

    def y_stage(n1, carry):
        for part in range(cols // 256):
            at = slice(part * 256, part * 256 + 256)
            at_im = slice(cols + part * 256, cols + part * 256 + 256)
            res = jnp.dot(ytab[n1], zed[n1, :, at], preferred_element_type=jnp.float32)
            res = res.astype(jnp.bfloat16)
            field[:, n1, :, at] = res[:short].reshape(chips, 16, 256)
            field[:, n1, :, at_im] = res[short:].reshape(chips, 16, 256)
        return carry

    lax.fori_loop(0, radix, y_stage, 0)

    pl.semaphore_wait(barrier, groups - 1)

    def energy_copy(i):
        return pltpu.make_async_remote_copy(
            src_ref=etile, dst_ref=eall.at[i], send_sem=e_s.at[i], recv_sem=e_r.at[i],
            device_id={"freq": lax.rem(me + i, groups)}, device_id_type=MESH,
        )

    def energy_start(i, carry):
        energy_copy(i).start()
        return carry

    lax.fori_loop(1, groups, energy_start, 0)

    def order(j):
        half = j // 2
        return jnp.where(lax.rem(j, 2) == 0, half, lines - 1 - half)

    def core_copy(a, b):
        return pltpu.make_async_remote_copy(
            src_ref=image.at[a, b, 1 - core], dst_ref=core_in.at[a, b],
            send_sem=core_s.at[a, b], recv_sem=core_r.at[a, b],
            device_id={"freq": core_peer}, device_id_type=MESH,
        )

    size = radix // pieces

    def pair_copy(a, p):
        cut = pl.ds(p * size, size)
        return pltpu.make_async_remote_copy(
            src_ref=image.at[a, 1 - pair, core, cut], dst_ref=pair_in.at[a, cut],
            send_sem=pair_s.at[a, p], recv_sem=pair_r.at[a, p],
            device_id={"freq": pair_peer}, device_id_type=MESH,
        )

    def low_copy(a, p):
        cut = pl.ds(p * size, size)
        return pltpu.make_async_remote_copy(
            src_ref=image.at[a, pair, core, cut], dst_ref=low_in.at[a, cut],
            send_sem=low_s.at[a, p], recv_sem=low_r.at[a, p],
            device_id={"freq": jnp.minimum(spot + 1, lines - 1) * 4 + pair * 2 + core},
            device_id_type=MESH,
        )

    def high_copy(a, p):
        cut = pl.ds(p * size, size)
        return pltpu.make_async_remote_copy(
            src_ref=image.at[a, pair, core, cut], dst_ref=high_in.at[a, cut],
            send_sem=high_s.at[a, p], recv_sem=high_r.at[a, p],
            device_id={"freq": jnp.maximum(spot - 1, 0) * 4 + pair * 2 + core},
            device_id_type=MESH,
        )

    def second(a):
        core_copy(a, 1 - pair).wait_recv()
        for p in range(pieces):
            cut = pl.ds(p * size, size)
            image[a, 1 - pair, core, cut] = (
                image[a, 1 - pair, core, cut] + core_in[a, 1 - pair, cut]
            )
            pair_copy(a, p).start()

    def compute(j, carry):
        a = order(j)
        lhs = field[pl.ds(2 * a, 2)].reshape(2 * radix * 16, 2 * cols)
        for part in range(cols // 256):
            at = slice(part * 256, part * 256 + 256)
            res = jnp.dot(lhs, xtab[:, at], preferred_element_type=jnp.float32)
            res = res.reshape(2, radix, 2, 8, 256)
            for c in range(2):
                image[a, :, c, :, :, at] = res[:, :, c]
        core_copy(a, 1 - pair).start()
        core_copy(a, pair).start()

        @pl.when(j > 0)
        def _():
            second(order(jnp.maximum(j - 1, 0)))

        return carry

    lax.fori_loop(0, lines, compute, 0)
    second(order(lines - 1))

    def third(j, carry):
        a = order(j)
        core_copy(a, pair).wait_recv()

        def piece(p, inner):
            cut = pl.ds(p * size, size)
            pair_copy(a, p).wait_recv()
            image[a, pair, core, cut] = (
                image[a, pair, core, cut] + core_in[a, pair, cut] + pair_in[a, cut]
            )

            @pl.when(jnp.logical_and(a >= spot, spot > 0))
            def _():
                low_copy(a, p).wait_recv()
                image[a, pair, core, cut] = image[a, pair, core, cut] + low_in[a, cut]

            @pl.when(jnp.logical_and(a <= spot, spot < lines - 1))
            def _():
                high_copy(a, p).wait_recv()
                image[a, pair, core, cut] = image[a, pair, core, cut] + high_in[a, cut]

            @pl.when(a > spot)
            def _():
                low_copy(a, p).start()

            @pl.when(a < spot)
            def _():
                high_copy(a, p).start()

            return inner

        return lax.fori_loop(0, pieces, piece, carry)

    lax.fori_loop(0, lines, third, 0)

    def energy_take(i, total):
        energy_copy(i).wait_recv()
        return total + eall[i]

    total = lax.fori_loop(1, groups, energy_take, etile[...])
    total = jnp.sum(jnp.sum(total, axis=0, keepdims=True), axis=1, keepdims=True)
    scale = lax.rsqrt(total / freq_total + 1e-06)
    out_ref[...] = image[spot, pair, core] * scale.reshape(1, 1, 1)

    def energy_end(i, carry):
        energy_copy(i).wait_send()
        return carry

    lax.fori_loop(1, groups, energy_end, 0)

    def finish(a, carry):
        core_copy(a, 0).wait_send()
        core_copy(a, 1).wait_send()

        def piece(p, inner):
            pair_copy(a, p).wait_send()

            @pl.when(a > spot)
            def _():
                low_copy(a, p).wait_send()

            @pl.when(a < spot)
            def _():
                high_copy(a, p).wait_send()

            return inner

        return lax.fori_loop(0, pieces, piece, carry)

    lax.fori_loop(0, lines, finish, 0)


def body(spectra, wavelet, freq_index, slowness, layer_ids, ray_slowness):
    slot_total, unused, rows, cols = spectra.shape
    groups = lax.axis_size("freq")
    freq_total = slot_total * groups
    radix = rows // groups // 8
    short = rows // radix
    lines = groups // 4
    pieces = min(4, radix)
    hertz = freq_index[0].astype(jnp.float32) * (FREQUENCY_BAND / freq_total) + LOW_FREQUENCY
    angular = hertz * (2.0 * math.pi)
    matches = jnp.arange(slowness.shape[0], dtype=jnp.int32) == layer_ids[0]
    slow = jnp.sum(jnp.where(matches, slowness, jnp.float32(0.0)))
    ray_x, ray_y = ray_slowness[0], ray_slowness[1]
    delay = jnp.sqrt(slow * slow - ray_x * ray_x - ray_y * ray_y) * DEPTH_STEP
    scal = jnp.stack(
        [
            (angular * angular - DAMPING * DAMPING) * slow * slow,
            2.0 * angular * DAMPING * slow * slow,
            hertz * ray_x * GRID_STEP,
            hertz * ray_y * GRID_STEP,
            hertz * delay,
            wavelet[0, 0],
            wavelet[0, 1],
            jnp.float32(freq_total),
        ]
    )
    f32, bf16 = jnp.float32, jnp.bfloat16
    dma = pltpu.SemaphoreType.DMA
    out = pl.pallas_call(
        functools.partial(kernel, groups, radix, pieces),
        out_shape=jax.ShapeDtypeStruct((radix, 8, cols), f32),
        in_specs=[
            pl.BlockSpec(memory_space=pltpu.SMEM),
            pl.BlockSpec(memory_space=pl.ANY),
        ],
        out_specs=pl.BlockSpec(memory_space=pltpu.VMEM),
        scratch_shapes=[
            pltpu.VMEM((2, radix, short, cols), bf16),
            pltpu.VMEM((radix, 2 * short, cols), bf16),
            pltpu.VMEM((radix, 2 * short, 2 * short), bf16),
            pltpu.VMEM((groups // 2, radix, 16, 2 * cols), bf16),
            pltpu.VMEM((2 * cols, cols), bf16),
            pltpu.VMEM((2, X_RADIX, cols), f32),
            pltpu.VMEM((lines, 2, 2, radix, 8, cols), f32),
            pltpu.VMEM((lines, 2, radix, 8, cols), f32),
            pltpu.VMEM((lines, radix, 8, cols), f32),
            pltpu.VMEM((lines, radix, 8, cols), f32),
            pltpu.VMEM((lines, radix, 8, cols), f32),
            pltpu.VMEM((8, LANES), f32),
            pltpu.VMEM((groups, 8, LANES), f32),
            dma((short // 16,)),
            dma((lines, 2)),
            dma((lines, 2)),
            dma((lines, pieces)),
            dma((lines, pieces)),
            dma((lines, pieces)),
            dma((lines, pieces)),
            dma((lines, pieces)),
            dma((lines, pieces)),
            dma((groups,)),
            dma((groups,)),
        ],
        compiler_params=pltpu.CompilerParams(
            collective_id=0, has_side_effects=True, vmem_limit_bytes=60 * 1024 * 1024
        ),
    )(scal, spectra[0].reshape(2, radix, short, cols))
    return out.transpose(1, 0, 2).reshape(1, 8 * radix, cols)


def solution(mesh):
    placed = (
        P(("rays", "freq"), None, None, None),
        P("freq", None),
        P("freq"),
        P(),
        P(),
        P("rays"),
    )
    return jax.shard_map(
        body, mesh=mesh, in_specs=placed, out_specs=P("rays", "freq", None), check_vma=False
    )
```

time: 194 us -> 90.8 us (0.47)
  the two profiles are of different devices: /device:TPU:0 before, /device:TPU:20 now
where the time goes in v1:
time: 90.8 us; the launch traced here: 90.5 us
  Pallas kernels  74.5 us (82%)
  between operations  8.47 us (9%)
  local copies, waits for them, and re-layouts  6.29 us (7%)
  other arithmetic  1.26 us (1%)
    pallas_call x1, Pallas kernels, body(): pl.pallas_call(functools.partial(kernel, groups, radix, pieces), out_shap...  74.5 us
    another operation x1, local copies, waits for them, and re-layouts, body(): jnp.stack([(angular * angular - DAMPING * DAMPING) * slow * slow, 2.0 * a...  1.85 us

profile of v1, /device:TPU:20, one launch (start us, length us, event | category | flops | bytes accessed | tf_op | source)
XLA Modules:
  0.0 90.5 jit_solution(12221880255614519874)
XLA Ops:
  1.3 1.3 %fusion = f32[]{:T(128)} fusion(f32[16]{0:T(128)} %param.9, s32[]{:T(128)} %bitcast.16), kind=kLoop, calls=%fused_computation.2 | loop fusion | flops 47 | bytes 72 | tf_op jit(solution)/shard_map/reduce_sum | solution.py:404
  5.9 1.3 %fusion.1 = (f32[1,1]{1,0:T(1,128)}, f32[1,1]{1,0:T(1,128)}) fusion(f32[1,2]{1,0:T(1,128)} %param.7), kind=kLoop, calls=%fused_computation.3 | loop fusion | bytes 16 | tf_op jit(solution)/shard_map/slice | solution.py:415
  7.2 1.3 %fusion.2 = (f32[1]{0:T(128)}, f32[1]{0:T(128)}) fusion(f32[2]{0:T(128)} %param.11), kind=kLoop, calls=%fused_computation.4 | loop fusion | bytes 16 | tf_op jit(solution)/shard_map/slice | solution.py:405
  12.4 1.9 %stack.23.scal = f32[8]{0:T(128)} concatenate(f32[1]{0:T(128)} %bitcast.2, f32[1]{0:T(128)} %bitcast.3, f32[1]{0:T(128)} %bitcast.5, f32[1]{0:T(128)} %bitcast.7, f32[1]{0:T(128)} %bitcast.8, f32[1]{0:T(128)} %bitcast.9, f32[1]{0:T(128)} %bitcast.10, f32[1]{0:T(128)} %constant.24.clone.1), dimensions={0} | concatenate | bytes 64 | tf_op jit(solution)/shard_map/stack | solution.py:407
  14.2 74.5 %shard_map.64 = f32[8,8,1024]{2,1,0:T(8,128)} custom-call(f32[8]{0:T(128)} %stack.23.scal, bf16[2,8,128,1024]{3,2,1,0:T(8,128)(2,1)} %bitcast.17), custom_call_target="tpu_custom_call" | custom-call | tf_op jit(solution)/shard_map/pallas_call | solution.py:421
  88.7 1.8 %copy.9 = f32[8,8,1024]{2,1,0:T(8,128)} copy(f32[8,8,1024]{2,0,1:T(8,128)} %bitcast.18) | data formatting | bytes 524288 | tf_op jit(solution)/shard_map/transpose | solution.py:459

commit v2 on v1

--- a/solution.py
+++ b/solution.py
@@ -15,20 +15,22 @@
 DAMPING = 6.0
 X_RADIX = 8
 LANES = 128
+LAG = 2
+DEPTH = 3
 MESH = pl.DeviceIdType.MESH
 
-SIN_COEFS = [(-1.0) ** i / math.factorial(2 * i + 1) for i in range(6)]
-COS_COEFS = [(-1.0) ** i / math.factorial(2 * i) for i in range(7)]
+SIN_COEFS = [(-1.0) ** i / math.factorial(2 * i + 1) for i in range(5)]
+COS_COEFS = [(-1.0) ** i / math.factorial(2 * i) for i in range(6)]
 
 
 def half_sincos(half):
     square = half * half
-    sine = jnp.full_like(square, SIN_COEFS[-1])
-    for coef in SIN_COEFS[-2::-1]:
+    sine = square * SIN_COEFS[-1] + SIN_COEFS[-2]
+    for coef in SIN_COEFS[-3::-1]:
         sine = sine * square + coef
     sine = sine * half
-    cosine = jnp.full_like(square, COS_COEFS[-1])
-    for coef in COS_COEFS[-2::-1]:
+    cosine = square * COS_COEFS[-1] + COS_COEFS[-2]
+    for coef in COS_COEFS[-3::-1]:
         cosine = cosine * square + coef
     twice = sine + sine
     return twice * cosine, 1.0 - twice * sine
@@ -69,8 +71,8 @@
 
 
 def kernel(
-    groups, radix, pieces,
-    scal, spec_hbm, out_ref,
+    groups, radix, pieces, freq_total,
+    wavelet, freq_index, slowness, layer_ids, rays, spec_hbm, out_ref,
     spec, zed, ytab, field, xtab, vecs, image, core_in, pair_in, low_in, high_in, etile, eall,
     load_sem, core_s, core_r, pair_s, pair_r, low_s, low_r, high_s, high_r, e_s, e_r,
 ):
@@ -110,14 +112,20 @@
 
     lax.fori_loop(0, strips, start_load, 0)
 
-    real_base = scal[0]
-    imag_arg = scal[1]
-    turn_x = scal[2]
-    turn_y = scal[3]
-    turn_0 = scal[4]
-    wave_re = scal[5]
-    wave_im = scal[6]
-    freq_total = scal[7]
+    hertz = freq_index[0, 0].astype(jnp.float32) * (FREQUENCY_BAND / freq_total) + LOW_FREQUENCY
+    angular = hertz * (2.0 * math.pi)
+    slow = slowness[layer_ids[0, 0]]
+    slow_sq = slow * slow
+    ray_x = rays[0]
+    ray_y = rays[1]
+    real_base = (angular * angular - DAMPING * DAMPING) * slow_sq
+    imag_arg = 2.0 * angular * DAMPING * slow_sq
+    turn_x = hertz * ray_x * GRID_STEP
+    turn_y = hertz * ray_y * GRID_STEP
+    vertical = jnp.full((16, LANES), slow_sq - ray_x * ray_x - ray_y * ray_y, jnp.float32)
+    turn_0 = jnp.sqrt(vertical) * (DEPTH_STEP * hertz)
+    wave_re = wavelet[0, 0]
+    wave_im = wavelet[0, 1]
 
     block = cols // X_RADIX
     place = lax.broadcasted_iota(jnp.int32, (X_RADIX, cols), 1)
@@ -288,14 +296,24 @@
             device_id_type=MESH,
         )
 
-    def second(a):
-        core_copy(a, 1 - pair).wait_recv()
-        for p in range(pieces):
-            cut = pl.ds(p * size, size)
-            image[a, 1 - pair, core, cut] = (
-                image[a, 1 - pair, core, cut] + core_in[a, 1 - pair, cut]
-            )
-            pair_copy(a, p).start()
+    count = lines * pieces
+    depth = min(DEPTH, count)
+
+    def split(i):
+        return order(i // pieces), lax.rem(i, pieces)
+
+    def send_pair(i):
+        a, p = split(i)
+        cut = pl.ds(p * size, size)
+
+        @pl.when(p == 0)
+        def _():
+            core_copy(a, 1 - pair).wait_recv()
+
+        image[a, 1 - pair, core, cut] = (
+            image[a, 1 - pair, core, cut] + core_in[a, 1 - pair, cut]
+        )
+        pair_copy(a, p).start()
 
     def compute(j, carry):
         a = order(j)
@@ -309,49 +327,65 @@
         core_copy(a, 1 - pair).start()
         core_copy(a, pair).start()
 
-        @pl.when(j > 0)
-        def _():
-            second(order(jnp.maximum(j - 1, 0)))
+        @pl.when(j == min(1, lines - 1))
+        def _():
+            for i in range(depth):
+                send_pair(i)
 
         return carry
 
     lax.fori_loop(0, lines, compute, 0)
-    second(order(lines - 1))
-
-    def third(j, carry):
-        a = order(j)
-        core_copy(a, pair).wait_recv()
-
-        def piece(p, inner):
+
+    def third(i, carry):
+        @pl.when(i < count)
+        def _():
+            a, p = split(jnp.minimum(i, count - 1))
             cut = pl.ds(p * size, size)
             pair_copy(a, p).wait_recv()
+
+            @pl.when(i + depth < count)
+            def _():
+                send_pair(jnp.minimum(i + depth, count - 1))
+
+            @pl.when(p == 0)
+            def _():
+                core_copy(a, pair).wait_recv()
+
             image[a, pair, core, cut] = (
                 image[a, pair, core, cut] + core_in[a, pair, cut] + pair_in[a, cut]
             )
 
-            @pl.when(jnp.logical_and(a >= spot, spot > 0))
+        upward = i - LAG * spot
+        a_up, p_up = split(jnp.clip(upward, 0, count - 1))
+
+        @pl.when((upward >= 0) & (upward < count) & (a_up > spot))
+        def _():
+            cut = pl.ds(p_up * size, size)
+
+            @pl.when(spot > 0)
             def _():
-                low_copy(a, p).wait_recv()
-                image[a, pair, core, cut] = image[a, pair, core, cut] + low_in[a, cut]
-
-            @pl.when(jnp.logical_and(a <= spot, spot < lines - 1))
+                low_copy(a_up, p_up).wait_recv()
+                image[a_up, pair, core, cut] = image[a_up, pair, core, cut] + low_in[a_up, cut]
+
+            low_copy(a_up, p_up).start()
+
+        downward = i - LAG * (lines - 1 - spot)
+        a_dn, p_dn = split(jnp.clip(downward, 0, count - 1))
+
+        @pl.when((downward >= 0) & (downward < count) & (a_dn < spot))
+        def _():
+            cut = pl.ds(p_dn * size, size)
+
+            @pl.when(spot < lines - 1)
             def _():
-                high_copy(a, p).wait_recv()
-                image[a, pair, core, cut] = image[a, pair, core, cut] + high_in[a, cut]
-
-            @pl.when(a > spot)
-            def _():
-                low_copy(a, p).start()
-
-            @pl.when(a < spot)
-            def _():
-                high_copy(a, p).start()
-
-            return inner
-
-        return lax.fori_loop(0, pieces, piece, carry)
-
-    lax.fori_loop(0, lines, third, 0)
+                high_copy(a_dn, p_dn).wait_recv()
+                image[a_dn, pair, core, cut] = image[a_dn, pair, core, cut] + high_in[a_dn, cut]
+
+            high_copy(a_dn, p_dn).start()
+
+        return carry
+
+    lax.fori_loop(0, count + LAG * (lines - 1), third, 0)
 
     def energy_take(i, total):
         energy_copy(i).wait_recv()
@@ -360,7 +394,25 @@
     total = lax.fori_loop(1, groups, energy_take, etile[...])
     total = jnp.sum(jnp.sum(total, axis=0, keepdims=True), axis=1, keepdims=True)
     scale = lax.rsqrt(total / freq_total + 1e-06)
-    out_ref[...] = image[spot, pair, core] * scale.reshape(1, 1, 1)
+
+    def own(p, carry):
+        cut = pl.ds(p * size, size)
+
+        @pl.when(spot > 0)
+        def _():
+            low_copy(spot, p).wait_recv()
+            image[spot, pair, core, cut] = image[spot, pair, core, cut] + low_in[spot, cut]
+
+        @pl.when(spot < lines - 1)
+        def _():
+            high_copy(spot, p).wait_recv()
+            image[spot, pair, core, cut] = image[spot, pair, core, cut] + high_in[spot, cut]
+
+        return carry
+
+    lax.fori_loop(0, pieces, own, 0)
+    for n1 in range(radix):
+        out_ref[:, n1, :] = image[spot, pair, core, n1] * scale
 
     def energy_end(i, carry):
         energy_copy(i).wait_send()
@@ -398,31 +450,13 @@
     short = rows // radix
     lines = groups // 4
     pieces = min(4, radix)
-    hertz = freq_index[0].astype(jnp.float32) * (FREQUENCY_BAND / freq_total) + LOW_FREQUENCY
-    angular = hertz * (2.0 * math.pi)
-    matches = jnp.arange(slowness.shape[0], dtype=jnp.int32) == layer_ids[0]
-    slow = jnp.sum(jnp.where(matches, slowness, jnp.float32(0.0)))
-    ray_x, ray_y = ray_slowness[0], ray_slowness[1]
-    delay = jnp.sqrt(slow * slow - ray_x * ray_x - ray_y * ray_y) * DEPTH_STEP
-    scal = jnp.stack(
-        [
-            (angular * angular - DAMPING * DAMPING) * slow * slow,
-            2.0 * angular * DAMPING * slow * slow,
-            hertz * ray_x * GRID_STEP,
-            hertz * ray_y * GRID_STEP,
-            hertz * delay,
-            wavelet[0, 0],
-            wavelet[0, 1],
-            jnp.float32(freq_total),
-        ]
-    )
     f32, bf16 = jnp.float32, jnp.bfloat16
     dma = pltpu.SemaphoreType.DMA
     out = pl.pallas_call(
-        functools.partial(kernel, groups, radix, pieces),
-        out_shape=jax.ShapeDtypeStruct((radix, 8, cols), f32),
+        functools.partial(kernel, groups, radix, pieces, freq_total),
+        out_shape=jax.ShapeDtypeStruct((8, radix, cols), f32),
         in_specs=[
-            pl.BlockSpec(memory_space=pltpu.SMEM),
+            *[pl.BlockSpec(memory_space=pltpu.SMEM)] * 5,
             pl.BlockSpec(memory_space=pl.ANY),
         ],
         out_specs=pl.BlockSpec(memory_space=pltpu.VMEM),
@@ -455,8 +489,11 @@
         compiler_params=pltpu.CompilerParams(
             collective_id=0, has_side_effects=True, vmem_limit_bytes=60 * 1024 * 1024
         ),
-    )(scal, spectra[0].reshape(2, radix, short, cols))
-    return out.transpose(1, 0, 2).reshape(1, 8 * radix, cols)
+    )(
+        wavelet, freq_index.reshape(1, 1), slowness, layer_ids.reshape(1, 1), ray_slowness,
+        spectra.reshape(2, radix, short, cols),
+    )
+    return out.reshape(1, 8 * radix, cols)
 
 
 def solution(mesh):

time: 90.8 us -> 59.8 us (0.66)
  the two profiles are of different devices: /device:TPU:20 before, /device:TPU:16 now
where the time goes in v2:
time: 59.8 us; the launch traced here: 59.6 us
  Pallas kernels  56.6 us (95%)
  local copies, waits for them, and re-layouts  1.67 us (3%)
  between operations  1.3 us (2%)
    pallas_call x1, Pallas kernels, body(): pl.pallas_call(functools.partial(kernel, groups, radix, pieces, freq_tota...  56.6 us
    unnamed x1, local copies, waits for them, and re-layouts  1.67 us

profile of v2, /device:TPU:16, one launch (start us, length us, event | category | flops | bytes accessed | tf_op | source)
XLA Modules:
  0.0 59.6 jit_solution(9896049910616015054)
XLA Ops:
  1.3 56.6 %shard_map.64 = f32[8,8,1024]{2,1,0:T(8,128)} custom-call(f32[1,2]{1,0:T(1,128)} %wavelet.1, s32[1,1]{1,0:T(1,128)} %bitcast.4.freq_index, f32[16]{0:T(128)} %slowness.1, s32[1,1]{1,0:T(1,128)} %bitcast.5.layer_ids, f32[2]{0:T(128)} %rays.1, bf16[2,8,128,1024]{3,2,1,0:T(8,128)(2,1)} %bitcast.6), custom_call_target="tpu_custom_call" | custom-call | tf_op jit(solution)/shard_map/pallas_call | solution.py:455
  57.9 1.7 %copy.10 = f32[1,64,1024]{2,1,0:T(8,128)} copy(f32[1,64,1024]{2,1,0:T(8,128)} %bitcast.7) | data formatting | bytes 524288

commit v3 on v2

--- a/solution.py
+++ b/solution.py
@@ -16,29 +16,37 @@
 X_RADIX = 8
 LANES = 128
 LAG = 2
-DEPTH = 3
+DEPTH = 4
+YTALL = 64
+EARLY = 2
 MESH = pl.DeviceIdType.MESH
 
-SIN_COEFS = [(-1.0) ** i / math.factorial(2 * i + 1) for i in range(5)]
-COS_COEFS = [(-1.0) ** i / math.factorial(2 * i) for i in range(6)]
-
-
-def half_sincos(half):
+PHASE_SIN = (0.9999998807907104, -0.16666465997695923, 0.008326363749802113, -0.00019062065985053778)
+PHASE_COS = (0.9999992251396179, -0.499982088804245, 0.04160428047180176, -0.0013190462486818433)
+TURN_SIN = (0.9999992251396179, -0.16665679216384888, 0.008313224650919437, -0.0001852344867074862)
+TURN_COS = (
+    0.9999999403953552, -0.4999990463256836, 0.041663579642772675, -0.0013853666605427861,
+    2.315317397005856e-05,
+)
+
+
+def polynomial(coefs, square):
+    value = square * coefs[-1] + coefs[-2]
+    for coef in coefs[-3::-1]:
+        value = value * square + coef
+    return value
+
+
+def half_sincos(half, sin_coefs, cos_coefs):
     square = half * half
-    sine = square * SIN_COEFS[-1] + SIN_COEFS[-2]
-    for coef in SIN_COEFS[-3::-1]:
-        sine = sine * square + coef
-    sine = sine * half
-    cosine = square * COS_COEFS[-1] + COS_COEFS[-2]
-    for coef in COS_COEFS[-3::-1]:
-        cosine = cosine * square + coef
+    sine = polynomial(sin_coefs, square) * half
     twice = sine + sine
-    return twice * cosine, 1.0 - twice * sine
+    return twice * polynomial(cos_coefs, square), 1.0 - twice * sine
 
 
 def turn_sincos(turns):
     reduced = turns - jnp.floor(turns + 0.5)
-    return half_sincos(reduced * math.pi)
+    return half_sincos(reduced * math.pi, TURN_SIN, TURN_COS)
 
 
 def butterfly(parts):
@@ -73,7 +81,7 @@
 def kernel(
     groups, radix, pieces, freq_total,
     wavelet, freq_index, slowness, layer_ids, rays, spec_hbm, out_ref,
-    spec, zed, ytab, field, xtab, vecs, image, core_in, pair_in, low_in, high_in, etile, eall,
+    spec, zed, ytab, field, xtab, vecs, ybase, image, core_in, pair_in, low_in, high_in, etile, eall,
     load_sem, core_s, core_r, pair_s, pair_r, low_s, low_r, high_s, high_r, e_s, e_r,
 ):
     rows = spec.shape[1] * spec.shape[2]
@@ -122,7 +130,7 @@
     imag_arg = 2.0 * angular * DAMPING * slow_sq
     turn_x = hertz * ray_x * GRID_STEP
     turn_y = hertz * ray_y * GRID_STEP
-    vertical = jnp.full((16, LANES), slow_sq - ray_x * ray_x - ray_y * ray_y, jnp.float32)
+    vertical = jnp.full((YTALL, LANES), slow_sq - ray_x * ray_x - ray_y * ray_y, jnp.float32)
     turn_0 = jnp.sqrt(vertical) * (DEPTH_STEP * hertz)
     wave_re = wavelet[0, 0]
     wave_im = wavelet[0, 1]
@@ -135,41 +143,50 @@
     vecs[0] = vec_cos
     vecs[1] = vec_sin
 
-    def x_table(step, carry):
-        strip = step // tiles
-        tile = lax.rem(step, tiles)
-        at = pl.ds(pl.multiple_of(tile * LANES, LANES), LANES)
-        k = lax.broadcasted_iota(jnp.int32, (16, LANES), 0) + strip * 16
-        x = lax.broadcasted_iota(jnp.int32, (16, LANES), 1) + tile * LANES
-        turns = lax.rem(k * x, cols).astype(jnp.float32) * (1.0 / cols)
-        sine, cosine = turn_sincos(turns)
-        for k1 in range(X_RADIX):
-            vc = vecs[0, k1 : k1 + 1, at]
-            vs = vecs[1, k1 : k1 + 1, at]
-            row = pl.ds(pl.multiple_of(strip * 16 + k1 * block, 16), 16)
-            row_im = pl.ds(pl.multiple_of(strip * 16 + k1 * block + cols, 16), 16)
-            xtab[row, at] = (cosine * vc - sine * vs).astype(jnp.bfloat16)
-            xtab[row_im, at] = (-(cosine * vs) - sine * vc).astype(jnp.bfloat16)
-        return carry
-
-    lax.fori_loop(0, (block // 16) * tiles, x_table, 0)
+    width = cols // pieces
+    deep = 32
+
+    def x_table(p):
+        at = pl.ds(pl.multiple_of(p * width, LANES), width)
+        x = lax.broadcasted_iota(jnp.int32, (deep, width), 1) + p * width
+        x = x.astype(jnp.float32) * (1.0 / cols)
+        k = lax.broadcasted_iota(jnp.int32, (deep, width), 0)
+
+        def strip_of(strip, carry):
+            sine, cosine = turn_sincos((k + strip * deep).astype(jnp.float32) * x)
+            for k1 in range(X_RADIX):
+                vc = vecs[0, k1 : k1 + 1, at]
+                vs = vecs[1, k1 : k1 + 1, at]
+                row = pl.ds(pl.multiple_of(strip * deep + k1 * block, deep), deep)
+                row_im = pl.ds(pl.multiple_of(strip * deep + k1 * block + cols, deep), deep)
+                xtab[row, at] = (cosine * vc - sine * vs).astype(jnp.bfloat16)
+                xtab[row_im, at] = (-(cosine * vs) - sine * vc).astype(jnp.bfloat16)
+            return carry
+
+        lax.fori_loop(0, block // deep, strip_of, 0)
+
+    x_table(0)
 
     ytiles = short // LANES
 
+    tall = short // YTALL
+
     def y_table(step, carry):
-        n1 = step // (strips * ytiles)
-        strip = lax.rem(step // ytiles, strips)
+        n1 = step // (tall * ytiles)
+        strip = lax.rem(step // ytiles, tall)
         tile = lax.rem(step, ytiles)
-        n2 = lax.broadcasted_iota(jnp.int32, (16, LANES), 0) + strip * 16
-        k2 = lax.broadcasted_iota(jnp.int32, (16, LANES), 1) + tile * LANES
+        n2 = lax.broadcasted_iota(jnp.int32, (YTALL, LANES), 0) + strip * YTALL
+        k2 = lax.broadcasted_iota(jnp.int32, (YTALL, LANES), 1) + tile * LANES
         n = n2 * radix + n1
-        turns = lax.rem(k2 * n, rows).astype(jnp.float32) * (1.0 / rows)
-        sine, cosine = turn_sincos(turns + n.astype(jnp.float32) * turn_y + turn_0)
+        n = n.astype(jnp.float32)
+        turns = k2.astype(jnp.float32) * (n * (1.0 / rows))
+        turns = turns - jnp.floor(turns)
+        sine, cosine = turn_sincos(turns + n * turn_y + turn_0)
         real = (wave_re * cosine + wave_im * sine).astype(jnp.bfloat16)
         imag_f = wave_re * sine - wave_im * cosine
         imag = imag_f.astype(jnp.bfloat16)
-        top = pl.ds(pl.multiple_of(strip * 16, 16), 16)
-        bottom = pl.ds(pl.multiple_of(strip * 16 + short, 16), 16)
+        top = pl.ds(pl.multiple_of(strip * YTALL, YTALL), YTALL)
+        bottom = pl.ds(pl.multiple_of(strip * YTALL + short, YTALL), YTALL)
         left = pl.ds(pl.multiple_of(tile * LANES, LANES), LANES)
         right = pl.ds(pl.multiple_of(tile * LANES + short, LANES), LANES)
         ytab[n1, top, left] = real
@@ -178,13 +195,19 @@
         ytab[n1, bottom, right] = real
         return carry
 
-    lax.fori_loop(0, radix * strips * ytiles, y_table, 0)
+    lax.fori_loop(0, radix * tall * ytiles, y_table, 0)
 
     step_y = 2.0 * math.pi / (rows * GRID_STEP)
     step_x = 2.0 * math.pi / (cols * GRID_STEP)
     imag_sq = imag_arg * imag_arg
     imag_half = imag_arg * 0.5
 
+    sub = lax.broadcasted_iota(jnp.int32, (short, LANES), 0)
+    for k1 in range(radix):
+        offset = k1 * short - (rows if k1 >= radix // 2 else 0)
+        ky = (sub + offset).astype(jnp.float32) * step_y
+        ybase[k1] = real_base - ky * ky
+
     def shift(strip, total):
         load(strip).wait()
         rows_at = pl.ds(pl.multiple_of(strip * 16, 16), 16)
@@ -193,13 +216,10 @@
             at = pl.ds(pl.multiple_of(tile * LANES, LANES), LANES)
             kx = lax.broadcasted_iota(jnp.int32, (16, LANES), 1) + tile * LANES
             kx = jnp.where(kx >= cols // 2, kx - cols, kx).astype(jnp.float32) * step_x
-            base = real_base - kx * kx
-            sub = lax.broadcasted_iota(jnp.int32, (16, LANES), 0) + strip * 16
+            kx_sq = kx * kx
             parts = []
             for k1 in range(radix):
-                offset = k1 * short - (rows if k1 >= radix // 2 else 0)
-                ky = (sub + offset).astype(jnp.float32) * step_y
-                a = base - ky * ky
+                a = ybase[k1, rows_at, :] - kx_sq
                 m = a * a + imag_sq
                 q = 0.5 * (m * lax.rsqrt(m) + jnp.abs(a))
                 iq = lax.rsqrt(q)
@@ -209,7 +229,9 @@
                 vert_re = jnp.where(forward, g, h)
                 vert_im = jnp.where(forward, h, g)
                 damp = jnp.exp(vert_im * -DEPTH_STEP)
-                sine, cosine = half_sincos(vert_re * (0.5 * DEPTH_STEP))
+                sine, cosine = half_sincos(
+                    vert_re * (0.5 * DEPTH_STEP), PHASE_SIN, PHASE_COS
+                )
                 cosine = cosine * damp
                 sine = sine * damp
                 re = spec[0, k1, rows_at, at].astype(jnp.float32)
@@ -261,36 +283,38 @@
         half = j // 2
         return jnp.where(lax.rem(j, 2) == 0, half, lines - 1 - half)
 
-    def core_copy(a, b):
+    def cut_of(p):
+        return pl.ds(pl.multiple_of(p * width, LANES), width)
+
+    def core_copy(p, b):
+        cut = cut_of(p)
         return pltpu.make_async_remote_copy(
-            src_ref=image.at[a, b, 1 - core], dst_ref=core_in.at[a, b],
-            send_sem=core_s.at[a, b], recv_sem=core_r.at[a, b],
+            src_ref=image.at[:, b, 1 - core, :, :, cut], dst_ref=core_in.at[:, b, :, :, cut],
+            send_sem=core_s.at[p, b], recv_sem=core_r.at[p, b],
             device_id={"freq": core_peer}, device_id_type=MESH,
         )
 
-    size = radix // pieces
-
     def pair_copy(a, p):
-        cut = pl.ds(p * size, size)
+        cut = cut_of(p)
         return pltpu.make_async_remote_copy(
-            src_ref=image.at[a, 1 - pair, core, cut], dst_ref=pair_in.at[a, cut],
+            src_ref=image.at[a, 1 - pair, core, :, :, cut], dst_ref=pair_in.at[a, :, :, cut],
             send_sem=pair_s.at[a, p], recv_sem=pair_r.at[a, p],
             device_id={"freq": pair_peer}, device_id_type=MESH,
         )
 
     def low_copy(a, p):
-        cut = pl.ds(p * size, size)
+        cut = cut_of(p)
         return pltpu.make_async_remote_copy(
-            src_ref=image.at[a, pair, core, cut], dst_ref=low_in.at[a, cut],
+            src_ref=image.at[a, pair, core, :, :, cut], dst_ref=low_in.at[a, :, :, cut],
             send_sem=low_s.at[a, p], recv_sem=low_r.at[a, p],
             device_id={"freq": jnp.minimum(spot + 1, lines - 1) * 4 + pair * 2 + core},
             device_id_type=MESH,
         )
 
     def high_copy(a, p):
-        cut = pl.ds(p * size, size)
+        cut = cut_of(p)
         return pltpu.make_async_remote_copy(
-            src_ref=image.at[a, pair, core, cut], dst_ref=high_in.at[a, cut],
+            src_ref=image.at[a, pair, core, :, :, cut], dst_ref=high_in.at[a, :, :, cut],
             send_sem=high_s.at[a, p], recv_sem=high_r.at[a, p],
             device_id={"freq": jnp.maximum(spot - 1, 0) * 4 + pair * 2 + core},
             device_id_type=MESH,
@@ -300,59 +324,41 @@
     depth = min(DEPTH, count)
 
     def split(i):
-        return order(i // pieces), lax.rem(i, pieces)
+        return order(lax.rem(i, lines)), i // lines
+
+    def first_of(i):
+        return lax.rem(i, lines) == 0
 
     def send_pair(i):
         a, p = split(i)
-        cut = pl.ds(p * size, size)
-
-        @pl.when(p == 0)
-        def _():
-            core_copy(a, 1 - pair).wait_recv()
-
-        image[a, 1 - pair, core, cut] = (
-            image[a, 1 - pair, core, cut] + core_in[a, 1 - pair, cut]
+        cut = cut_of(p)
+
+        @pl.when(first_of(i))
+        def _():
+            core_copy(p, 1 - pair).wait_recv()
+
+        image[a, 1 - pair, core, :, :, cut] = (
+            image[a, 1 - pair, core, :, :, cut] + core_in[a, 1 - pair, :, :, cut]
         )
         pair_copy(a, p).start()
-
-    def compute(j, carry):
-        a = order(j)
-        lhs = field[pl.ds(2 * a, 2)].reshape(2 * radix * 16, 2 * cols)
-        for part in range(cols // 256):
-            at = slice(part * 256, part * 256 + 256)
-            res = jnp.dot(lhs, xtab[:, at], preferred_element_type=jnp.float32)
-            res = res.reshape(2, radix, 2, 8, 256)
-            for c in range(2):
-                image[a, :, c, :, :, at] = res[:, :, c]
-        core_copy(a, 1 - pair).start()
-        core_copy(a, pair).start()
-
-        @pl.when(j == min(1, lines - 1))
-        def _():
-            for i in range(depth):
-                send_pair(i)
-
-        return carry
-
-    lax.fori_loop(0, lines, compute, 0)
 
     def third(i, carry):
         @pl.when(i < count)
         def _():
             a, p = split(jnp.minimum(i, count - 1))
-            cut = pl.ds(p * size, size)
+            cut = cut_of(p)
             pair_copy(a, p).wait_recv()
 
             @pl.when(i + depth < count)
             def _():
                 send_pair(jnp.minimum(i + depth, count - 1))
 
-            @pl.when(p == 0)
+            @pl.when(first_of(i))
             def _():
-                core_copy(a, pair).wait_recv()
-
-            image[a, pair, core, cut] = (
-                image[a, pair, core, cut] + core_in[a, pair, cut] + pair_in[a, cut]
+                core_copy(p, pair).wait_recv()
+
+            image[a, pair, core, :, :, cut] = (
+                image[a, pair, core, :, :, cut] + core_in[a, pair, :, :, cut] + pair_in[a, :, :, cut]
             )
 
         upward = i - LAG * spot
@@ -360,12 +366,12 @@
 
         @pl.when((upward >= 0) & (upward < count) & (a_up > spot))
         def _():
-            cut = pl.ds(p_up * size, size)
+            cut = cut_of(p_up)
 
             @pl.when(spot > 0)
             def _():
                 low_copy(a_up, p_up).wait_recv()
-                image[a_up, pair, core, cut] = image[a_up, pair, core, cut] + low_in[a_up, cut]
+                image[a_up, pair, core, :, :, cut] = image[a_up, pair, core, :, :, cut] + low_in[a_up, :, :, cut]
 
             low_copy(a_up, p_up).start()
 
@@ -374,18 +380,44 @@
 
         @pl.when((downward >= 0) & (downward < count) & (a_dn < spot))
         def _():
-            cut = pl.ds(p_dn * size, size)
+            cut = cut_of(p_dn)
 
             @pl.when(spot < lines - 1)
             def _():
                 high_copy(a_dn, p_dn).wait_recv()
-                image[a_dn, pair, core, cut] = image[a_dn, pair, core, cut] + high_in[a_dn, cut]
+                image[a_dn, pair, core, :, :, cut] = image[a_dn, pair, core, :, :, cut] + high_in[a_dn, :, :, cut]
 
             high_copy(a_dn, p_dn).start()
 
         return carry
 
-    lax.fori_loop(0, count + LAG * (lines - 1), third, 0)
+    def compute(p, carry):
+        at = cut_of(p)
+
+        @pl.when(p > 0)
+        def _():
+            x_table(p)
+
+        @pl.when(p == 1)
+        def _():
+            lax.fori_loop(0, depth, lambda i, c: (send_pair(i), c)[1], 0)
+
+        lax.fori_loop(EARLY * jnp.maximum(p - 2, 0), EARLY * jnp.maximum(p - 1, 0), third, 0)
+
+        half = max(lines // 4, 1)
+        for q in range(lines // half):
+            lhs = field[2 * half * q : 2 * half * (q + 1)].reshape(half * 2 * radix * 16, 2 * cols)
+            res = jnp.dot(lhs, xtab[:, at], preferred_element_type=jnp.float32)
+            res = res.reshape(half, 2, radix, 2, 8, width)
+            for c in range(2):
+                image[half * q : half * (q + 1), :, c, :, :, at] = res[:, :, :, c]
+        core_copy(p, 1 - pair).start()
+        core_copy(p, pair).start()
+        return carry
+
+    lax.fori_loop(0, pieces, compute, 0)
+
+    lax.fori_loop(EARLY * max(pieces - 2, 0), count + LAG * (lines - 1), third, 0)
 
     def energy_take(i, total):
         energy_copy(i).wait_recv()
@@ -396,17 +428,17 @@
     scale = lax.rsqrt(total / freq_total + 1e-06)
 
     def own(p, carry):
-        cut = pl.ds(p * size, size)
+        cut = cut_of(p)
 
         @pl.when(spot > 0)
         def _():
             low_copy(spot, p).wait_recv()
-            image[spot, pair, core, cut] = image[spot, pair, core, cut] + low_in[spot, cut]
+            image[spot, pair, core, :, :, cut] = image[spot, pair, core, :, :, cut] + low_in[spot, :, :, cut]
 
         @pl.when(spot < lines - 1)
         def _():
             high_copy(spot, p).wait_recv()
-            image[spot, pair, core, cut] = image[spot, pair, core, cut] + high_in[spot, cut]
+            image[spot, pair, core, :, :, cut] = image[spot, pair, core, :, :, cut] + high_in[spot, :, :, cut]
 
         return carry
 
@@ -420,10 +452,14 @@
 
     lax.fori_loop(1, groups, energy_end, 0)
 
+    def finish_core(p, carry):
+        core_copy(p, 0).wait_send()
+        core_copy(p, 1).wait_send()
+        return carry
+
+    lax.fori_loop(0, pieces, finish_core, 0)
+
     def finish(a, carry):
-        core_copy(a, 0).wait_send()
-        core_copy(a, 1).wait_send()
-
         def piece(p, inner):
             pair_copy(a, p).wait_send()
 
@@ -449,7 +485,7 @@
     radix = rows // groups // 8
     short = rows // radix
     lines = groups // 4
-    pieces = min(4, radix)
+    pieces = min(4, cols // LANES)
     f32, bf16 = jnp.float32, jnp.bfloat16
     dma = pltpu.SemaphoreType.DMA
     out = pl.pallas_call(
@@ -467,6 +503,7 @@
             pltpu.VMEM((groups // 2, radix, 16, 2 * cols), bf16),
             pltpu.VMEM((2 * cols, cols), bf16),
             pltpu.VMEM((2, X_RADIX, cols), f32),
+            pltpu.VMEM((radix, short, LANES), f32),
             pltpu.VMEM((lines, 2, 2, radix, 8, cols), f32),
             pltpu.VMEM((lines, 2, radix, 8, cols), f32),
             pltpu.VMEM((lines, radix, 8, cols), f32),
@@ -475,8 +512,8 @@
             pltpu.VMEM((8, LANES), f32),
             pltpu.VMEM((groups, 8, LANES), f32),
             dma((short // 16,)),
-            dma((lines, 2)),
-            dma((lines, 2)),
+            dma((pieces, 2)),
+            dma((pieces, 2)),
             dma((lines, pieces)),
             dma((lines, pieces)),
             dma((lines, pieces)),

time: 59.8 us -> 57.1 us (0.955)
  the two profiles are of different devices: /device:TPU:16 before, /device:TPU:0 now
where the time goes in v3:
time: 57.1 us; the launch traced here: 56.9 us
  Pallas kernels  54 us (95%)
  local copies, waits for them, and re-layouts  1.67 us (3%)
  between operations  1.3 us (2%)
    pallas_call x1, Pallas kernels, body(): pl.pallas_call(functools.partial(kernel, groups, radix, pieces, freq_tota...  54 us
    unnamed x1, local copies, waits for them, and re-layouts  1.67 us

profile of v3, /device:TPU:0, one launch (start us, length us, event | category | flops | bytes accessed | tf_op | source)
XLA Modules:
  0.0 56.9 jit_solution(13629759932362695705)
XLA Ops:
  1.3 54.0 %shard_map.64 = f32[8,8,1024]{2,1,0:T(8,128)} custom-call(f32[1,2]{1,0:T(1,128)} %wavelet.1, s32[1,1]{1,0:T(1,128)} %bitcast.4.freq_index, f32[16]{0:T(128)} %slowness.1, s32[1,1]{1,0:T(1,128)} %bitcast.5.layer_ids, f32[2]{0:T(128)} %rays.1, bf16[2,8,128,1024]{3,2,1,0:T(8,128)(2,1)} %bitcast.6), custom_call_target="tpu_custom_call" | custom-call | tf_op jit(solution)/shard_map/pallas_call | solution.py:491
  55.3 1.7 %copy.10 = f32[1,64,1024]{2,1,0:T(8,128)} copy(f32[1,64,1024]{2,1,0:T(8,128)} %bitcast.7) | data formatting | bytes 524288

commit v4 on v3

--- a/solution.py
+++ b/solution.py
@@ -163,7 +163,7 @@
                 xtab[row_im, at] = (-(cosine * vs) - sine * vc).astype(jnp.bfloat16)
             return carry
 
-        lax.fori_loop(0, block // deep, strip_of, 0)
+        lax.fori_loop(0, block // deep, strip_of, 0, unroll=True)
 
     x_table(0)
 
@@ -195,7 +195,7 @@
         ytab[n1, bottom, right] = real
         return carry
 
-    lax.fori_loop(0, radix * tall * ytiles, y_table, 0)
+    lax.fori_loop(0, radix * tall * ytiles, y_table, 0, unroll=2)
 
     step_y = 2.0 * math.pi / (rows * GRID_STEP)
     step_x = 2.0 * math.pi / (cols * GRID_STEP)
@@ -246,7 +246,7 @@
                 zed[n1, low, at] = im.astype(jnp.bfloat16)
             return acc
 
-        return lax.fori_loop(0, tiles, inner, total)
+        return lax.fori_loop(0, tiles, inner, total, unroll=2)
 
     energy = lax.fori_loop(0, strips, shift, jnp.zeros((16, LANES), jnp.float32))
     etile[...] = energy[:8] + energy[8:]
@@ -263,7 +263,7 @@
             field[:, n1, :, at_im] = res[short:].reshape(chips, 16, 256)
         return carry
 
-    lax.fori_loop(0, radix, y_stage, 0)
+    lax.fori_loop(0, radix, y_stage, 0, unroll=True)
 
     pl.semaphore_wait(barrier, groups - 1)
 

time: 57.1 us -> 55.4 us (0.970)
  Pallas kernels: 54 us -> 52.3 us
    pallas_call x1, Pallas kernels: 54 us -> 52.3 us  [body(): pl.pallas_call(functools.partial(kernel, groups, radix, pieces, freq_tota...]
where the time goes in v4:
time: 55.4 us; the launch traced here: 55.3 us
  Pallas kernels  52.3 us (94%)
  local copies, waits for them, and re-layouts  1.67 us (3%)
  between operations  1.3 us (2%)
    pallas_call x1, Pallas kernels, body(): pl.pallas_call(functools.partial(kernel, groups, radix, pieces, freq_tota...  52.3 us
    unnamed x1, local copies, waits for them, and re-layouts  1.67 us

profile of v4, /device:TPU:0, one launch (start us, length us, event | category | flops | bytes accessed | tf_op | source)
XLA Modules:
  0.0 55.3 jit_solution(1960859113248202471)
XLA Ops:
  1.3 52.3 %shard_map.64 = f32[8,8,1024]{2,1,0:T(8,128)} custom-call(f32[1,2]{1,0:T(1,128)} %wavelet.1, s32[1,1]{1,0:T(1,128)} %bitcast.4.freq_index, f32[16]{0:T(128)} %slowness.1, s32[1,1]{1,0:T(1,128)} %bitcast.5.layer_ids, f32[2]{0:T(128)} %rays.1, bf16[2,8,128,1024]{3,2,1,0:T(8,128)(2,1)} %bitcast.6), custom_call_target="tpu_custom_call" | custom-call | tf_op jit(solution)/shard_map/pallas_call | solution.py:491
  53.6 1.7 %copy.10 = f32[1,64,1024]{2,1,0:T(8,128)} copy(f32[1,64,1024]{2,1,0:T(8,128)} %bitcast.7) | data formatting | bytes 524288
